TPU v7x, 128 devices: a whole 4x4x4 slice. The times are simulated.
128 devices in a mesh: section: 4 (over z), dp: 8 (over y, core), mp: 4 (over x).
Axes of the slice: x: 4, y: 4, z: 4, core: 2. Of those that a mesh axis runs over, the one named last changes fastest.
Arguments:
- text: bfloat16 [4, 4096, 4096], P('section', ('dp', 'mp')), may hold values from -6 to 6
- patches: bfloat16 [16384, 1024], P(('section', 'dp')), may hold values from -6 to 6
- segments: int32 [4, 8, 512], P('section', 'dp'), may hold values from 0 to 3, never falling along the last dimension, each value on 1 to 256 neighbouring positions
- loss_mask: int32 [4, 4096], P('section', ('dp', 'mp')), may hold values from 0 to 1, as said below
- tile_batch: int32 [8, 8], P('dp'), may hold values from 0 to 3, as said below
- tile_offset: int32 [8, 8], P('dp'), may hold values from 0 to 448, as said below
- attn_gain: float32 [4, 4096], P('section'), may hold values from 0.5 to 2
- w_query: bfloat16 [4, 4096, 2048], P('section', None, 'mp'), may hold values from -0.09375 to 0.09375
- w_kv: bfloat16 [4, 2, 4096, 512], P('section', None, None, 'mp'), may hold values from -0.09375 to 0.09375
- w_out: bfloat16 [4, 2048, 4096], P('section', 'mp'), may hold values from -0.125 to 0.125
- vis_gain: float32 [2, 1024], replicated, may hold values from 0.5 to 2
- vis_bias: float32 [2, 1024], replicated, may hold values from -3 to 3
- v_qkv: bfloat16 [3, 1024, 1024], P(None, ('section', 'dp'), 'mp'), may hold values from -0.1875 to 0.1875
- v_out: bfloat16 [1024, 1024], P('mp', ('section', 'dp')), may hold values from -0.1875 to 0.1875
- v_up: bfloat16 [1024, 4096], P(('section', 'dp'), 'mp'), may hold values from -0.1875 to 0.1875
- v_down: bfloat16 [4096, 1024], P('mp', ('section', 'dp')), may hold values from -0.09375 to 0.09375
- v_proj: bfloat16 [4096, 4096], P(('section', 'dp'), 'mp'), may hold values from -0.09375 to 0.09375
Outputs:
- hidden: bfloat16 [4, 4096, 4096], P('section', ('dp', 'mp'))
- token_weight: float32 [4, 4096], P('section', ('dp', 'mp'))
Inputs may be any that keep to these rules, and one draw needn't show every extreme that they name: `tile_batch`: in every data-parallel index, the 2 tiles of each section index go 1 to each of two different micro-batches; one micro-batch receives 1 tiles from every section index. `tile_offset`: offsets are multiples of 64; the runs of one sequence never intersect. `loss_mask`: the first position of every sequence is a one.
All inputs are finite; a program needn't handle non-finite values.
Results may differ from a plain program's by a relative error of at most 0.025.
Values may be sent and summed in bfloat16 or wider, within the bound.
A program may use at most 192 MiB of HBM per device.

v0:
```python
import jax
import jax.numpy as jnp
from jax import lax
from jax.sharding import Mesh
from jax.sharding import PartitionSpec as P

HD = 128
VHD = 64
GRID = 16
PATCH = 256
POOL = 64
SECTION_DP = ("section", "dp_0", "dp_1")
SECTION_DP_MP = ("section", "dp_0", "dp_1", "mp")
DP = ("dp_0", "dp_1")
DP_MP = ("dp_0", "dp_1", "mp")
EPS = 1e-05
ROPE_BASE = 500000.0
BLOCKED = -1e30


def copy_for_each(array, axis):
    copies = jnp.broadcast_to(array, (lax.axis_size(axis), *array.shape))
    return lax.all_to_all(copies, axis, split_axis=0, concat_axis=0, tiled=True)


def over_copies(array, axis):
    everything = copy_for_each(array, axis)
    return jnp.sum(everything.astype(jnp.float32), axis=0)


def laid_out(tiles, dim):
    lengths = list(tiles.shape[1:])
    lengths[dim] *= tiles.shape[0]
    return jnp.moveaxis(tiles, 0, dim).reshape(lengths)


def one_gather(arrays, axis, dims):
    flat = jnp.concatenate([a.reshape(-1) for a in arrays])
    lines, at, done = (lax.all_gather(flat, axis), 0, [])
    for a, dim in zip(arrays, dims):
        tiles = lines[:, at : at + a.size].reshape(-1, *a.shape)
        done.append(laid_out(tiles, dim))
        at += a.size
    return tuple(done)


def shifted(value, axis, steps):
    count = lax.axis_size(axis)
    pairs = [(source, (source + steps) % count) for source in range(count)]
    return lax.ppermute(value, axis, pairs)


def over_axes(array, axes):
    for axis in axes:
        array = lax.psum(array, axis)
    return array


def layer_norm(values, gain, bias):
    wide = values.astype(jnp.float32)
    center = wide - jnp.mean(wide, axis=-1, keepdims=True)
    spread = jnp.mean(center * center, axis=-1, keepdims=True)
    return (center * lax.rsqrt(spread + EPS) * gain + bias).astype(jnp.bfloat16)


def rms_norm(values, gain):
    wide = values.astype(jnp.float32)
    power = jnp.mean(wide * wide, axis=-1, keepdims=True)
    return (wide * lax.rsqrt(power + EPS) * gain).astype(jnp.bfloat16)


def rotate(values, positions):
    half_width = values.shape[-1] // 2
    freqs = ROPE_BASE ** (-2.0 * jnp.arange(half_width, dtype=jnp.float32) / values.shape[-1])
    angles = positions.astype(jnp.float32)[:, None] * freqs[None, :]
    cosine = jnp.cos(angles)[:, None, :]
    sinus_part = jnp.sin(angles)[:, None, :]
    first_half = values[..., :half_width]
    second_half = values[..., half_width:]
    return jnp.concatenate(
        [
            first_half * cosine - second_half * sinus_part,
            second_half * cosine + first_half * sinus_part,
        ],
        axis=-1,
    )


def pixel_shuffle(states):
    tile_count = states.shape[0] // PATCH
    side_half = GRID // 2
    width = states.shape[1]
    arranged = states.reshape(tile_count, side_half, 2, side_half, 2, width)
    return arranged.transpose(0, 1, 3, 2, 4, 5).reshape(
        tile_count * side_half * side_half, 4 * width
    )


def block_sum(partial_value):
    return over_copies(partial_value.astype(jnp.bfloat16), "mp").astype(jnp.float32)


def encode_tiles(patches, vis_gain, vis_bias, qkv_full, out_full, up_full, down_full, proj_full):
    tile_count = patches.shape[0] // PATCH
    local_width = qkv_full.shape[2]
    head_count = local_width // VHD
    normed = layer_norm(patches, vis_gain[0], vis_bias[0])
    projected = [
        jnp.dot(normed, qkv_full[index], preferred_element_type=jnp.float32)
        .astype(jnp.bfloat16)
        .reshape(tile_count, PATCH, head_count, VHD)
        for index in range(3)
    ]
    scores = jnp.einsum(
        "tqhd,tkhd->thqk", projected[0], projected[1], preferred_element_type=jnp.float32
    ) * VHD ** (-0.5)
    probs = jax.nn.softmax(scores, axis=-1).astype(jnp.bfloat16)
    mixed = (
        jnp.einsum("thqk,tkhd->tqhd", probs, projected[2], preferred_element_type=jnp.float32)
        .astype(jnp.bfloat16)
        .reshape(tile_count * PATCH, local_width)
    )
    attended = block_sum(jnp.dot(mixed, out_full, preferred_element_type=jnp.float32))
    residual = (patches.astype(jnp.float32) + attended).astype(jnp.bfloat16)
    normed_two = layer_norm(residual, vis_gain[1], vis_bias[1])
    inner = jax.nn.gelu(
        jnp.dot(normed_two, up_full, preferred_element_type=jnp.float32), approximate=False
    ).astype(jnp.bfloat16)
    fed = block_sum(jnp.dot(inner, down_full, preferred_element_type=jnp.float32))
    states = (residual.astype(jnp.float32) + fed).astype(jnp.bfloat16)
    return jnp.dot(pixel_shuffle(states), proj_full, preferred_element_type=jnp.float32).astype(
        jnp.bfloat16
    )


def decoder_layer(active, state, segment_ids, gain, w_query, w_kv, w_out):
    normed = rms_norm(state, gain)
    query_width = w_query.shape[1]
    pair_width = w_kv.shape[2]
    joined_width = query_width + 2 * pair_width
    model_width = w_out.shape[1]
    piece = lax.all_gather(normed, "mp", axis=0, tiled=True)
    row_count = piece.shape[0]

    def project_computed(rows):
        positions = jnp.arange(row_count, dtype=jnp.int32)
        query = jnp.dot(rows, w_query, preferred_element_type=jnp.float32).reshape(
            row_count, query_width // HD, HD
        )
        keyed = jnp.dot(rows, w_kv[0], preferred_element_type=jnp.float32).reshape(
            row_count, pair_width // HD, HD
        )
        valued = jnp.dot(rows, w_kv[1], preferred_element_type=jnp.float32)
        return jnp.concatenate(
            [
                rotate(query, positions).reshape(row_count, query_width),
                rotate(keyed, positions).reshape(row_count, pair_width),
                valued,
            ],
            axis=1,
        ).astype(jnp.bfloat16)

    def project_skipped(rows):
        return jnp.zeros((row_count, joined_width), jnp.bfloat16)

    joined = lax.cond(active, project_computed, project_skipped, piece)
    length = joined.shape[0]
    pair_heads = pair_width // HD
    group_size = query_width // pair_width

    def attend(joined_rows):
        query = joined_rows[:, :query_width].reshape(length, pair_heads, group_size, HD)
        keyed = joined_rows[:, query_width : query_width + pair_width].reshape(
            length, pair_heads, HD
        )
        valued = joined_rows[:, query_width + pair_width :].reshape(length, pair_heads, HD)
        scores = jnp.einsum(
            "qkgd,skd->kgqs", query, keyed, preferred_element_type=jnp.float32
        ) * HD ** (-0.5)
        row_ids = jnp.arange(length, dtype=jnp.int32)
        allowed = (segment_ids[:, None] == segment_ids[None, :]) & (
            row_ids[None, :] <= row_ids[:, None]
        )
        scores = jnp.where(allowed, scores, BLOCKED)
        probs = jax.nn.softmax(scores, axis=-1).astype(jnp.bfloat16)
        return (
            jnp.einsum("kgqs,skd->qkgd", probs, valued, preferred_element_type=jnp.float32)
            .astype(jnp.bfloat16)
            .reshape(length, query_width)
        )

    def attend_skipped(joined_rows):
        return jnp.zeros((length, query_width), jnp.bfloat16)

    mixed = lax.cond(active, attend, attend_skipped, joined)
    count = state.shape[0] * lax.axis_size("mp")

    def out_computed(values):
        return jnp.dot(values, w_out, preferred_element_type=jnp.float32)

    def out_skipped(values):
        return jnp.zeros((count, model_width), jnp.float32)

    summed = lax.psum_scatter(
        lax.cond(active, out_computed, out_skipped, mixed).astype(jnp.bfloat16),
        "mp",
        scatter_dimension=0,
        tiled=True,
    ).astype(jnp.float32)
    updated = (state.astype(jnp.float32) + summed).astype(jnp.bfloat16)
    return jnp.where(active, updated, state)


def shards(
    text,
    patches,
    segments,
    loss_mask,
    tile_batch,
    tile_offset,
    attn_gain,
    w_query,
    w_kv,
    w_out,
    vis_gain,
    vis_bias,
    v_qkv,
    v_out,
    v_up,
    v_down,
    v_proj,
):
    sections = lax.axis_size("section")
    section_at = lax.axis_index("section")
    part_at = lax.axis_index("mp")
    qkv_full, out_full, up_full, down_full, proj_full = one_gather(
        (v_qkv, v_out, v_up, v_down, v_proj), SECTION_DP, (1, 1, 0, 1, 0)
    )
    embedded = encode_tiles(
        patches, vis_gain, vis_bias, qkv_full, out_full, up_full, down_full, proj_full
    )
    length = segments.shape[2]
    tiles_here = embedded.shape[0] // POOL
    batch_all = tile_batch[0]
    offset_all = tile_offset[0]
    own_batch = lax.dynamic_slice_in_dim(batch_all, section_at * tiles_here, tiles_here, 0)
    capacity = tiles_here // 2
    block_rows = capacity * POOL
    local_ids = jnp.arange(tiles_here, dtype=jnp.int32)
    local_same = (own_batch[:, None] == own_batch[None, :]) & (
        local_ids[None, :] < local_ids[:, None]
    )
    local_rank = jnp.sum(local_same.astype(jnp.int32), axis=1)
    send_rows = jnp.arange(sections * block_rows, dtype=jnp.int32)
    send_target = send_rows // block_rows
    send_rank = send_rows % block_rows // POOL
    send_match = (own_batch[None, :] == send_target[:, None]) & (
        local_rank[None, :] == send_rank[:, None]
    )
    own_rows = jnp.arange(tiles_here * POOL, dtype=jnp.int32)
    send_pick = jnp.repeat(send_match, POOL, axis=1) & (
        (own_rows % POOL)[None, :] == (send_rows % POOL)[:, None]
    )
    blocks = jnp.dot(
        send_pick.astype(jnp.bfloat16), embedded, preferred_element_type=jnp.float32
    ).astype(jnp.bfloat16)
    arrived = lax.all_to_all(blocks, "section", split_axis=0, concat_axis=0, tiled=True)
    tile_ids = jnp.arange(batch_all.shape[0], dtype=jnp.int32)
    source_ids = tile_ids // tiles_here
    tile_same = (
        (batch_all[:, None] == batch_all[None, :])
        & (source_ids[:, None] == source_ids[None, :])
        & (tile_ids[None, :] < tile_ids[:, None])
    )
    tile_rank = jnp.sum(tile_same.astype(jnp.int32), axis=1)
    slot_rows = jnp.arange(sections * block_rows, dtype=jnp.int32)
    slot_source = slot_rows // block_rows
    slot_rank = slot_rows % block_rows // POOL
    match = (
        (batch_all[None, :] == section_at)
        & (source_ids[None, :] == slot_source[:, None])
        & (tile_rank[None, :] == slot_rank[:, None])
    )
    slot_place = jnp.sum(match.astype(jnp.int32) * offset_all[None, :], axis=1) + slot_rows % POOL
    slot_valid = jnp.any(match, axis=1)
    places = jnp.arange(length, dtype=jnp.int32)
    picker = ((places[:, None] == slot_place[None, :]) & slot_valid[None, :]).astype(jnp.bfloat16)
    image_cols = jnp.dot(picker, arrived, preferred_element_type=jnp.float32).astype(jnp.bfloat16)
    image_rows = lax.all_to_all(image_cols, "mp", split_axis=0, concat_axis=1, tiled=True)
    shard_rows = image_rows.shape[0]
    positions = part_at * shard_rows + jnp.arange(shard_rows, dtype=jnp.int32)
    covered = jnp.any(
        (batch_all[None, :] == section_at)
        & (positions[:, None] >= offset_all[None, :])
        & (positions[:, None] < offset_all[None, :] + POOL),
        axis=1,
    )
    start_state = jnp.where(covered[:, None], image_rows, text[0])
    gain_here = attn_gain[0]
    query_here = w_query[0]
    pair_here = w_kv[0]
    out_here = w_out[0]
    state = start_state
    segment_ids = segments[0, 0]
    for tick_index in range(2 * sections):
        if tick_index < 2 * sections - 1:
            micro_at = jnp.mod(section_at - tick_index, sections)
            begin_at = jnp.mod(sections - micro_at, sections)
            active = (tick_index >= begin_at) & (tick_index < begin_at + sections)
            state = decoder_layer(
                active, state, segment_ids, gain_here, query_here, pair_here, out_here
            )
        state, segment_ids = shifted((state, segment_ids), "section", 1)
    totals = over_axes(jnp.sum(loss_mask), SECTION_DP_MP)
    scaling = float(sections * lax.axis_size(DP) * length)
    token_weight = loss_mask.astype(jnp.float32) * scaling / totals.astype(jnp.float32)
    return (state[None], token_weight)


def solution(mesh):
    split = Mesh(
        mesh.devices.reshape(mesh.shape["section"], 4, 2, mesh.shape["mp"]),
        ("section", "dp_0", "dp_1", "mp"),
    )
    return jax.shard_map(
        shards,
        mesh=split,
        in_specs=(
            P("section", DP_MP, None),
            P(SECTION_DP, None),
            P("section", DP, None),
            P("section", DP_MP),
            P(DP, None),
            P(DP, None),
            P("section", None),
            P("section", None, "mp"),
            P("section", None, None, "mp"),
            P("section", "mp", None),
            P(),
            P(),
            P(None, SECTION_DP, "mp"),
            P("mp", SECTION_DP),
            P(SECTION_DP, "mp"),
            P("mp", SECTION_DP),
            P(SECTION_DP, "mp"),
        ),
        out_specs=(P("section", DP_MP, None), P("section", DP_MP)),
        check_vma=False,
    )
```

profile of v0, /device:TPU:32, one launch (start us, length us, event | category | flops | bytes accessed | tf_op | source)
XLA Modules:
  0.0 1387.6 jit_solution(4361427265575410445)
XLA Ops:
  16.4 66.2 %all-gather.24.cloned.1.call-done = bf16[7340032]{0:T(1024)(128)(2,1)} async-done(((bf16[229376]{0:T(1024)(128)(2,1)}), bf16[7340032]{0:T(1024)(128)(2,1)}) %all-gather.24.cloned.1.call-update) | async-done | bytes 14680080 | tf_op jit(solution)/shard_map/all_gather | solution.py:39
  82.6 13.2 reshape.1320
  141.0 27.2 %all-to-all-done = bf16[4,512,1024]{2,1,0:T(8,128)(2,1)} async-done(((bf16[4,512,1024]{2,1,0:T(8,128)(2,1)}), bf16[4,512,1024]{2,1,0:T(8,128)(2,1)}, u32[]{:S(2)}, u32[]{:S(2)}) %all-to-all-start) | async-done | bytes 4194336 | tf_op jit(solution)/shard_map/all_to_all | solution.py:23
  205.8 31.9 %all-to-all-done.1 = bf16[4,512,1024]{2,1,0:T(8,128)(2,1)} async-done(((bf16[4,512,1024]{2,1,0:T(8,128)(2,1)}), bf16[4,512,1024]{2,1,0:T(8,128)(2,1)}, u32[]{:S(2)}, u32[]{:S(2)}) %all-to-all-start.1) | async-done | bytes 4194336 | tf_op jit(solution)/shard_map/all_to_all | solution.py:23
  268.5 11.0 all-to-all-done.3
  285.6 46.9 %all-gather.10.cloned.1.call-done = bf16[512,4096]{1,0:T(8,128)(2,1)} async-done(((bf16[128,4096]{1,0:T(8,128)(2,1)}), bf16[512,4096]{1,0:T(8,128)(2,1)}) %all-gather.10.cloned.1.call-update) | async-done | bytes 4194320 | tf_op jit(solution)/shard_map/all_gather | solution.py:142
  341.9 62.8 %reduce-scatter.8.cloned.1.call-done = bf16[128,4096]{1,0:T(8,128)(2,1)} async-done(((bf16[512,4096]{1,0:T(8,128)(2,1)}), bf16[128,4096]{1,0:T(8,128)(2,1)}) %reduce-scatter.8.cloned.1.call-update) | async-done | bytes 1048592 | tf_op jit(solution)/shard_map/reduce_scatter | solution.py:204
  408.5 23.3 %collective-permute-done = bf16[128,4096]{1,0:T(8,128)(2,1)S(1)} collective-permute-done((bf16[128,4096]{1,0:T(8,128)(2,1)S(1)}, bf16[128,4096]{1,0:T(8,128)(2,1)S(1)}, u32[]{:S(2)}, u32[]{:S(2)}) %collective-permute-start) | collective-permute-done | bytes 1048608 | tf_op jit(solution)/shard_map/ppermute | solution.py:50
  435.0 46.4 %all-gather.12.cloned.1.call-done = bf16[512,4096]{1,0:T(8,128)(2,1)} async-done(((bf16[128,4096]{1,0:T(8,128)(2,1)}), bf16[512,4096]{1,0:T(8,128)(2,1)}) %all-gather.12.cloned.1.call-update) | async-done | bytes 4194320 | tf_op jit(solution)/shard_map/all_gather | solution.py:142
  491.6 10.4 conditional.25
  509.2 45.7 %reduce-scatter.10.cloned.1.call-done = bf16[128,4096]{1,0:T(8,128)(2,1)} async-done(((bf16[512,4096]{1,0:T(8,128)(2,1)}), bf16[128,4096]{1,0:T(8,128)(2,1)}) %reduce-scatter.10.cloned.1.call-update) | async-done | bytes 1048592 | tf_op jit(solution)/shard_map/reduce_scatter | solution.py:204
  558.0 23.3 %collective-permute-done.2 = bf16[128,4096]{1,0:T(8,128)(2,1)S(1)} collective-permute-done((bf16[128,4096]{1,0:T(8,128)(2,1)S(1)}, bf16[128,4096]{1,0:T(8,128)(2,1)S(1)}, u32[]{:S(2)}, u32[]{:S(2)}) %collective-permute-start.2) | collective-permute-done | bytes 1048608 | tf_op jit(solution)/shard_map/ppermute | solution.py:50
  584.6 46.4 %all-gather.14.cloned.1.call-done = bf16[512,4096]{1,0:T(8,128)(2,1)} async-done(((bf16[128,4096]{1,0:T(8,128)(2,1)}), bf16[512,4096]{1,0:T(8,128)(2,1)}) %all-gather.14.cloned.1.call-update) | async-done | bytes 4194320 | tf_op jit(solution)/shard_map/all_gather | solution.py:142
  641.2 10.6 conditional.28
  658.6 47.3 %reduce-scatter.12.cloned.1.call-done = bf16[128,4096]{1,0:T(8,128)(2,1)} async-done(((bf16[512,4096]{1,0:T(8,128)(2,1)}), bf16[128,4096]{1,0:T(8,128)(2,1)}) %reduce-scatter.12.cloned.1.call-update) | async-done | bytes 1048592 | tf_op jit(solution)/shard_map/reduce_scatter | solution.py:204
  709.0 23.3 %collective-permute-done.4 = bf16[128,4096]{1,0:T(8,128)(2,1)S(1)} collective-permute-done((bf16[128,4096]{1,0:T(8,128)(2,1)S(1)}, bf16[128,4096]{1,0:T(8,128)(2,1)S(1)}, u32[]{:S(2)}, u32[]{:S(2)}) %collective-permute-start.4) | collective-permute-done | bytes 1048608 | tf_op jit(solution)/shard_map/ppermute | solution.py:50
  735.6 46.4 %all-gather.16.cloned.1.call-done = bf16[512,4096]{1,0:T(8,128)(2,1)} async-done(((bf16[128,4096]{1,0:T(8,128)(2,1)}), bf16[512,4096]{1,0:T(8,128)(2,1)}) %all-gather.16.cloned.1.call-update) | async-done | bytes 4194320 | tf_op jit(solution)/shard_map/all_gather | solution.py:142
  782.0 10.4 conditional.30
  792.3 10.5 conditional.31
  810.0 46.8 %reduce-scatter.14.cloned.1.call-done = bf16[128,4096]{1,0:T(8,128)(2,1)} async-done(((bf16[512,4096]{1,0:T(8,128)(2,1)}), bf16[128,4096]{1,0:T(8,128)(2,1)}) %reduce-scatter.14.cloned.1.call-update) | async-done | bytes 1048592 | tf_op jit(solution)/shard_map/reduce_scatter | solution.py:204
  860.0 23.3 %collective-permute-done.6 = bf16[128,4096]{1,0:T(8,128)(2,1)S(1)} collective-permute-done((bf16[128,4096]{1,0:T(8,128)(2,1)S(1)}, bf16[128,4096]{1,0:T(8,128)(2,1)S(1)}, u32[]{:S(2)}, u32[]{:S(2)}) %collective-permute-start.6) | collective-permute-done | bytes 1048608 | tf_op jit(solution)/shard_map/ppermute | solution.py:50
  886.6 46.4 %all-gather.18.cloned.1.call-done = bf16[512,4096]{1,0:T(8,128)(2,1)} async-done(((bf16[128,4096]{1,0:T(8,128)(2,1)}), bf16[512,4096]{1,0:T(8,128)(2,1)}) %all-gather.18.cloned.1.call-update) | async-done | bytes 4194320 | tf_op jit(solution)/shard_map/all_gather | solution.py:142
  943.1 10.5 conditional.34
  960.5 47.3 %reduce-scatter.16.cloned.1.call-done = bf16[128,4096]{1,0:T(8,128)(2,1)} async-done(((bf16[512,4096]{1,0:T(8,128)(2,1)}), bf16[128,4096]{1,0:T(8,128)(2,1)}) %reduce-scatter.16.cloned.1.call-update) | async-done | bytes 1048592 | tf_op jit(solution)/shard_map/reduce_scatter | solution.py:204
  1011.0 23.3 %collective-permute-done.8 = bf16[128,4096]{1,0:T(8,128)(2,1)S(1)} collective-permute-done((bf16[128,4096]{1,0:T(8,128)(2,1)S(1)}, bf16[128,4096]{1,0:T(8,128)(2,1)S(1)}, u32[]{:S(2)}, u32[]{:S(2)}) %collective-permute-start.8) | collective-permute-done | bytes 1048608 | tf_op jit(solution)/shard_map/ppermute | solution.py:50
  1037.5 46.4 %all-gather.20.cloned.1.call-done = bf16[512,4096]{1,0:T(8,128)(2,1)} async-done(((bf16[128,4096]{1,0:T(8,128)(2,1)}), bf16[512,4096]{1,0:T(8,128)(2,1)}) %all-gather.20.cloned.1.call-update) | async-done | bytes 4194320 | tf_op jit(solution)/shard_map/all_gather | solution.py:142
  1088.5 70.3 %reduce-scatter.18.cloned.1.call-done = bf16[128,4096]{1,0:T(8,128)(2,1)} async-done(((bf16[512,4096]{1,0:T(8,128)(2,1)}), bf16[128,4096]{1,0:T(8,128)(2,1)}) %reduce-scatter.18.cloned.1.call-update) | async-done | bytes 1048592 | tf_op jit(solution)/shard_map/reduce_scatter | solution.py:204
  1161.9 23.3 %collective-permute-done.10 = bf16[128,4096]{1,0:T(8,128)(2,1)S(1)} collective-permute-done((bf16[128,4096]{1,0:T(8,128)(2,1)S(1)}, bf16[128,4096]{1,0:T(8,128)(2,1)S(1)}, u32[]{:S(2)}, u32[]{:S(2)}) %collective-permute-start.10) | collective-permute-done | bytes 1048608 | tf_op jit(solution)/shard_map/ppermute | solution.py:50
  1188.5 46.4 %all-gather.22.cloned.1.call-done = bf16[512,4096]{1,0:T(8,128)(2,1)} async-done(((bf16[128,4096]{1,0:T(8,128)(2,1)}), bf16[512,4096]{1,0:T(8,128)(2,1)}) %all-gather.22.cloned.1.call-update) | async-done | bytes 4194320 | tf_op jit(solution)/shard_map/all_gather | solution.py:142
  1237.8 65.9 %reduce-scatter.20.cloned.1.call-done = bf16[128,4096]{1,0:T(8,128)(2,1)} async-done(((bf16[512,4096]{1,0:T(8,128)(2,1)}), bf16[128,4096]{1,0:T(8,128)(2,1)}) %reduce-scatter.20.cloned.1.call-update) | async-done | bytes 1048592 | tf_op jit(solution)/shard_map/reduce_scatter | solution.py:204
  1306.9 23.3 %collective-permute-done.12 = bf16[128,4096]{1,0:T(8,128)(2,1)S(1)} collective-permute-done((bf16[128,4096]{1,0:T(8,128)(2,1)S(1)}, bf16[128,4096]{1,0:T(8,128)(2,1)S(1)}, u32[]{:S(2)}, u32[]{:S(2)}) %collective-permute-start.12) | collective-permute-done | bytes 1048608 | tf_op jit(solution)/shard_map/ppermute | solution.py:50
  1332.3 26.3 %psum.28 = s32[]{:T(128)} all-reduce(s32[]{:T(128)} %reduce_sum.242), channel_id=1, replica_groups=mesh['section'=4,'dp_0'=4,'dp_1'=2,'mp'=4] {'section'}, use_global_device_ids=true, to_apply=%region_84.85 | all-reduce | flops 1 | bytes 8 | tf_op jit(solution)/shard_map/psum | solution.py:55
  (310 shorter events, 389.6 us)
Async XLA Ops:
  7.2 75.4 %all-gather.24.cloned.1.call-start = ((), (), s32[]{:S(2)}) async-start(), calls=%async_computation.25 | async-start | bytes 15138816 | tf_op jit(solution)/shard_map/all_gather | solution.py:39
  113.6 54.6 %all-to-all-start = ((bf16[4,512,1024]{2,1,0:T(8,128)(2,1)}), bf16[4,512,1024]{2,1,0:T(8,128)(2,1)}, u32[]{:S(2)}, u32[]{:S(2)}) async-start(bf16[4,512,1024]{2,1,0:T(8,128)(2,1)} %broadcast_in_dim.76), calls=%async_computation | async-start | bytes 8388608 | tf_op jit(solution)/shard_map/all_to_all | solution.py:23
  183.6 54.1 %all-to-all-start.1 = ((bf16[4,512,1024]{2,1,0:T(8,128)(2,1)}), bf16[4,512,1024]{2,1,0:T(8,128)(2,1)}, u32[]{:S(2)}, u32[]{:S(2)}) async-start(bf16[4,512,1024]{2,1,0:T(8,128)(2,1)} %broadcast_in_dim.85), calls=%async_computation.1 | async-start | bytes 8388608 | tf_op jit(solution)/shard_map/all_to_all | solution.py:23
  262.4 17.1 %all-to-all-start.3 = ((bf16[4,128,1024]{2,1,0:T(8,128)(2,1)}), bf16[4,128,1024]{2,1,0:T(8,128)(2,1)}, u32[]{:S(2)}, u32[]{:S(2)}) async-start(bf16[4,128,1024]{2,1,0:T(8,128)(2,1)} %bitcast.135), calls=%async_computation.3 | async-start | bytes 2097152 | tf_op jit(solution)/shard_map/all_to_all | solution.py:289
  266.8 65.7 %all-gather.10.cloned.1.call-start = ((), (), s32[]{:S(2)}) async-start(), calls=%async_computation.11 | async-start | bytes 5242880 | tf_op jit(solution)/shard_map/all_gather | solution.py:142
  285.5 119.2 %reduce-scatter.8.cloned.1.call-start = ((), (), s32[]{:S(2)}) async-start(), calls=%async_computation.12 | async-start | bytes 5242880 | tf_op jit(solution)/shard_map/reduce_scatter | solution.py:204
  336.9 144.5 %all-gather.12.cloned.1.call-start = ((), (), s32[]{:S(2)}) async-start(), calls=%async_computation.13 | async-start | bytes 5242880 | tf_op jit(solution)/shard_map/all_gather | solution.py:142
  406.8 24.9 %collective-permute-start = (bf16[128,4096]{1,0:T(8,128)(2,1)S(1)}, bf16[128,4096]{1,0:T(8,128)(2,1)S(1)}, u32[]{:S(2)}, u32[]{:S(2)}) collective-permute-start(bf16[128,4096]{1,0:T(8,128)(2,1)S(1)} %fusion.241), channel_id=1, source_target_pairs={{0,32},{32,64},{64,96},{96,0},{1,33},{33,65},{65,97},{97,1},{2,34}... | collective-permute-start | bytes 3145736 | tf_op jit(solution)/shard_map/ppermute | solution.py:50
  433.4 121.5 %reduce-scatter.10.cloned.1.call-start = ((), (), s32[]{:S(2)}) async-start(), calls=%async_computation.14 | async-start | bytes 5242880 | tf_op jit(solution)/shard_map/reduce_scatter | solution.py:204
  433.4 58.2 %collective-permute-start.1 = (s32[512]{0:T(512)S(1)}, s32[512]{0:T(512)S(1)}, u32[]{:S(2)}, u32[]{:S(2)}) collective-permute-start(s32[512]{0:T(512)S(1)} %bitcast.536), channel_id=1, source_target_pairs={{0,32},{32,64},{64,96},{96,0},{1,33},{33,65},{65,97},{97,1},{2,34}... | collective-permute-start | bytes 6152 | tf_op jit(solution)/shard_map/ppermute | solution.py:50
  509.2 121.9 %all-gather.14.cloned.1.call-start = ((), (), s32[]{:S(2)}) async-start(), calls=%async_computation.15 | async-start | bytes 5242880 | tf_op jit(solution)/shard_map/all_gather | solution.py:142
  556.4 24.9 %collective-permute-start.2 = (bf16[128,4096]{1,0:T(8,128)(2,1)S(1)}, bf16[128,4096]{1,0:T(8,128)(2,1)S(1)}, u32[]{:S(2)}, u32[]{:S(2)}) collective-permute-start(bf16[128,4096]{1,0:T(8,128)(2,1)S(1)} %fusion.240), channel_id=1, source_target_pairs={{0,32},{32,64},{64,96},{96,0},{1,33},{33,65},{65,97},{97,1},{2,34}... | collective-permute-start | bytes 3145736 | tf_op jit(solution)/shard_map/ppermute | solution.py:50
  583.0 122.9 %reduce-scatter.12.cloned.1.call-start = ((), (), s32[]{:S(2)}) async-start(), calls=%async_computation.16 | async-start | bytes 5242880 | tf_op jit(solution)/shard_map/reduce_scatter | solution.py:204
  583.0 58.2 %collective-permute-start.3 = (s32[512]{0:T(512)S(1)}, s32[512]{0:T(512)S(1)}, u32[]{:S(2)}, u32[]{:S(2)}) collective-permute-start(s32[512]{0:T(512)S(1)} %collective-permute-done.1), channel_id=1, source_target_pairs={{0,32},{32,64},{64,96},{96,0},{1,33},{33,65},{65,97},{97,1},{2,34}... | collective-permute-start | bytes 6152 | tf_op jit(solution)/shard_map/ppermute | solution.py:50
  658.5 123.4 %all-gather.16.cloned.1.call-start = ((), (), s32[]{:S(2)}) async-start(), calls=%async_computation.17 | async-start | bytes 5242880 | tf_op jit(solution)/shard_map/all_gather | solution.py:142
  707.3 24.9 %collective-permute-start.4 = (bf16[128,4096]{1,0:T(8,128)(2,1)S(1)}, bf16[128,4096]{1,0:T(8,128)(2,1)S(1)}, u32[]{:S(2)}, u32[]{:S(2)}) collective-permute-start(bf16[128,4096]{1,0:T(8,128)(2,1)S(1)} %fusion.239), channel_id=1, source_target_pairs={{0,32},{32,64},{64,96},{96,0},{1,33},{33,65},{65,97},{97,1},{2,34}... | collective-permute-start | bytes 3145736 | tf_op jit(solution)/shard_map/ppermute | solution.py:50
  733.9 122.9 %reduce-scatter.14.cloned.1.call-start = ((), (), s32[]{:S(2)}) async-start(), calls=%async_computation.18 | async-start | bytes 5242880 | tf_op jit(solution)/shard_map/reduce_scatter | solution.py:204
  733.9 58.4 %collective-permute-start.5 = (s32[512]{0:T(512)S(1)}, s32[512]{0:T(512)S(1)}, u32[]{:S(2)}, u32[]{:S(2)}) collective-permute-start(s32[512]{0:T(512)S(1)} %collective-permute-done.3), channel_id=1, source_target_pairs={{0,32},{32,64},{64,96},{96,0},{1,33},{33,65},{65,97},{97,1},{2,34}... | collective-permute-start | bytes 6152 | tf_op jit(solution)/shard_map/ppermute | solution.py:50
  809.5 123.4 %all-gather.18.cloned.1.call-start = ((), (), s32[]{:S(2)}) async-start(), calls=%async_computation.19 | async-start | bytes 5242880 | tf_op jit(solution)/shard_map/all_gather | solution.py:142
  858.4 24.9 %collective-permute-start.6 = (bf16[128,4096]{1,0:T(8,128)(2,1)S(1)}, bf16[128,4096]{1,0:T(8,128)(2,1)S(1)}, u32[]{:S(2)}, u32[]{:S(2)}) collective-permute-start(bf16[128,4096]{1,0:T(8,128)(2,1)S(1)} %fusion.238), channel_id=1, source_target_pairs={{0,32},{32,64},{64,96},{96,0},{1,33},{33,65},{65,97},{97,1},{2,34}... | collective-permute-start | bytes 3145736 | tf_op jit(solution)/shard_map/ppermute | solution.py:50
  884.9 122.9 %reduce-scatter.16.cloned.1.call-start = ((), (), s32[]{:S(2)}) async-start(), calls=%async_computation.20 | async-start | bytes 5242880 | tf_op jit(solution)/shard_map/reduce_scatter | solution.py:204
  884.9 58.2 %collective-permute-start.7 = (s32[512]{0:T(512)S(1)}, s32[512]{0:T(512)S(1)}, u32[]{:S(2)}, u32[]{:S(2)}) collective-permute-start(s32[512]{0:T(512)S(1)} %collective-permute-done.5), channel_id=1, source_target_pairs={{0,32},{32,64},{64,96},{96,0},{1,33},{33,65},{65,97},{97,1},{2,34}... | collective-permute-start | bytes 6152 | tf_op jit(solution)/shard_map/ppermute | solution.py:50
  960.5 123.4 %all-gather.20.cloned.1.call-start = ((), (), s32[]{:S(2)}) async-start(), calls=%async_computation.21 | async-start | bytes 5242880 | tf_op jit(solution)/shard_map/all_gather | solution.py:142
  1009.3 24.9 %collective-permute-start.8 = (bf16[128,4096]{1,0:T(8,128)(2,1)S(1)}, bf16[128,4096]{1,0:T(8,128)(2,1)S(1)}, u32[]{:S(2)}, u32[]{:S(2)}) collective-permute-start(bf16[128,4096]{1,0:T(8,128)(2,1)S(1)} %fusion.237), channel_id=1, source_target_pairs={{0,32},{32,64},{64,96},{96,0},{1,33},{33,65},{65,97},{97,1},{2,34}... | collective-permute-start | bytes 3145736 | tf_op jit(solution)/shard_map/ppermute | solution.py:50
  1035.9 122.9 %reduce-scatter.18.cloned.1.call-start = ((), (), s32[]{:S(2)}) async-start(), calls=%async_computation.22 | async-start | bytes 5242880 | tf_op jit(solution)/shard_map/reduce_scatter | solution.py:204
  1035.9 48.9 %collective-permute-start.9 = (s32[512]{0:T(512)S(1)}, s32[512]{0:T(512)S(1)}, u32[]{:S(2)}, u32[]{:S(2)}) collective-permute-start(s32[512]{0:T(512)S(1)} %collective-permute-done.7), channel_id=1, source_target_pairs={{0,32},{32,64},{64,96},{96,0},{1,33},{33,65},{65,97},{97,1},{2,34}... | collective-permute-start | bytes 6152 | tf_op jit(solution)/shard_map/ppermute | solution.py:50
  1088.4 146.5 %all-gather.22.cloned.1.call-start = ((), (), s32[]{:S(2)}) async-start(), calls=%async_computation.23 | async-start | bytes 5242880 | tf_op jit(solution)/shard_map/all_gather | solution.py:142
  1160.3 24.9 %collective-permute-start.10 = (bf16[128,4096]{1,0:T(8,128)(2,1)S(1)}, bf16[128,4096]{1,0:T(8,128)(2,1)S(1)}, u32[]{:S(2)}, u32[]{:S(2)}) collective-permute-start(bf16[128,4096]{1,0:T(8,128)(2,1)S(1)} %fusion.236), channel_id=1, source_target_pairs={{0,32},{32,64},{64,96},{96,0},{1,33},{33,65},{65,97},{97,1},{2,34}... | collective-permute-start | bytes 3145736 | tf_op jit(solution)/shard_map/ppermute | solution.py:50
  1186.8 116.9 %reduce-scatter.20.cloned.1.call-start = ((), (), s32[]{:S(2)}) async-start(), calls=%async_computation.24 | async-start | bytes 5242880 | tf_op jit(solution)/shard_map/reduce_scatter | solution.py:204
  1186.9 48.3 %collective-permute-start.11 = (s32[512]{0:T(512)S(1)}, s32[512]{0:T(512)S(1)}, u32[]{:S(2)}, u32[]{:S(2)}) collective-permute-start(s32[512]{0:T(512)S(1)} %collective-permute-done.9), channel_id=1, source_target_pairs={{0,32},{32,64},{64,96},{96,0},{1,33},{33,65},{65,97},{97,1},{2,34}... | collective-permute-start | bytes 6152 | tf_op jit(solution)/shard_map/ppermute | solution.py:50
  1305.3 24.9 %collective-permute-start.12 = (bf16[128,4096]{1,0:T(8,128)(2,1)S(1)}, bf16[128,4096]{1,0:T(8,128)(2,1)S(1)}, u32[]{:S(2)}, u32[]{:S(2)}) collective-permute-start(bf16[128,4096]{1,0:T(8,128)(2,1)S(1)} %fusion.235), channel_id=1, source_target_pairs={{0,32},{32,64},{64,96},{96,0},{1,33},{33,65},{65,97},{97,1},{2,34}... | collective-permute-start | bytes 3145736 | tf_op jit(solution)/shard_map/ppermute | solution.py:50
  1330.1 49.6 %collective-permute-start.13 = (bf16[128,4096]{1,0:T(8,128)(2,1)S(1)}, bf16[128,4096]{1,0:T(8,128)(2,1)S(1)}, u32[]{:S(2)}, u32[]{:S(2)}) collective-permute-start(bf16[128,4096]{1,0:T(8,128)(2,1)S(1)} %collective-permute-done.12), channel_id=1, source_target_pairs={{0,32},{32,64},{64,96},{96,0},{1,33},{33,65},{65,97},{97,1},{2,34}... | collective-permute-start | bytes 3145736 | tf_op jit(solution)/shard_map/ppermute | solution.py:50
  (26 other events, 291.0 us)
Sparse Core Ops, SparseCore 0:
  13.2 69.3 all-gather.23
  285.6 46.8 all-gather.9
  337.1 67.6 reduce-scatter.7
  433.5 47.9 all-gather.11
  509.3 45.5 reduce-scatter.9
  583.1 47.8 all-gather.13
  658.6 47.1 reduce-scatter.11
  734.0 47.8 all-gather.15
  809.6 47.1 reduce-scatter.13
  885.0 47.9 all-gather.17
  960.6 47.1 reduce-scatter.15
  1036.0 47.8 all-gather.19
  1088.5 70.1 reduce-scatter.17
  1187.0 47.8 all-gather.21
  1237.9 65.7 reduce-scatter.19
where the time goes:
time: 1400 us; the launch traced here: 1390 us
  waiting for transfers between devices  1020 us (73%)
  local copies, waits for them, and re-layouts  106 us (8%)
  matrix products  101 us (7%)
  other arithmetic  51.4 us (4%)
  starting transfers between devices  48.4 us (3%)
  blocking collectives  46.2 us (3%)
  between operations  15.6 us (1%)
    reduce_scatter x7, waiting for transfers between devices, decoder_layer(): lax.psum_scatter(lax.cond(active, out_computed, out_skipped, mixed).astyp...  386 us
    all_gather x7, waiting for transfers between devices, decoder_layer(): piece = lax.all_gather(normed, 'mp', axis=0, tiled=True)  325 us
    ppermute x14, waiting for transfers between devices, shifted(): return lax.ppermute(value, axis, pairs)  163 us
    all_gather x1, waiting for transfers between devices, one_gather(): lines, at, done = (lax.all_gather(flat, axis), 0, [])  66.2 us
    all_to_all x2, waiting for transfers between devices, copy_for_each(): return lax.all_to_all(copies, axis, split_axis=0, concat_axis=0, tiled=True)  59.1 us
    psum x4, blocking collectives, over_axes(): array = lax.psum(array, axis)  46.2 us
  transfers between devices with their start and end apart: 33, of which 26 were waited for; matrix products, arithmetic and copies ran while one was open for 6% of the time, Pallas kernels for 0%

commit v1 on v0

--- a/solution.py
+++ b/solution.py
@@ -16,6 +16,14 @@
 EPS = 1e-05
 ROPE_BASE = 500000.0
 BLOCKED = -1e30
+
+
+def gather_by_exchange(array, axis, dim):
+    length = lax.axis_size(axis)
+    repeats = [length if d == dim else 1 for d in range(array.ndim)]
+    return lax.all_to_all(
+        jnp.tile(array, repeats), axis, split_axis=dim, concat_axis=dim, tiled=True
+    )
 
 
 def copy_for_each(array, axis):
@@ -139,7 +147,7 @@
     pair_width = w_kv.shape[2]
     joined_width = query_width + 2 * pair_width
     model_width = w_out.shape[1]
-    piece = lax.all_gather(normed, "mp", axis=0, tiled=True)
+    piece = gather_by_exchange(normed, "mp", 0)
     row_count = piece.shape[0]
 
     def project_computed(rows):

time: 1400 us -> 1460 us (1.043)
  starting transfers between devices: 48.4 us -> 76.8 us
  local copies, waits for them, and re-layouts: 106 us -> 127 us
  matrix products: 101 us -> 119 us
    all_gather x7 -> x0, waiting for transfers between devices: 325 us -> none  [decoder_layer(): piece = lax.all_gather(normed, 'mp', axis=0, tiled=True)]
    all_to_all x0 -> x7, waiting for transfers between devices: none -> 318 us  [gather_by_exchange(): lax.all_to_all(jnp.tile(array, repeats), axis, split_axis=dim, concat_axi...]
    all_to_all x0 -> x7, starting transfers between devices: none -> 34.1 us  [gather_by_exchange(): lax.all_to_all(jnp.tile(array, repeats), axis, split_axis=dim, concat_axi...]
    another operation x13 -> x20, local copies, waits for them, and re-layouts: 20.2 us -> 37.9 us
  transfers between devices with their start and end apart: 33 -> 33, of which waited for: 26 -> 26; matrix products, arithmetic and copies ran while one was open for 6% -> 8% of each run, Pallas kernels for 0% -> 0%
where the time goes in v1:
time: 1460 us; the launch traced here: 1450 us
  waiting for transfers between devices  1020 us (70%)
  local copies, waits for them, and re-layouts  127 us (9%)
  matrix products  119 us (8%)
  starting transfers between devices  76.8 us (5%)
  blocking collectives  46.2 us (3%)
  other arithmetic  43 us (3%)
  between operations  16 us (1%)
    reduce_scatter x7, waiting for transfers between devices, decoder_layer(): lax.psum_scatter(lax.cond(active, out_computed, out_skipped, mixed).astyp...  400 us
    all_to_all x7, waiting for transfers between devices, gather_by_exchange(): lax.all_to_all(jnp.tile(array, repeats), axis, split_axis=dim, concat_axi...  318 us
    ppermute x14, waiting for transfers between devices, shifted(): return lax.ppermute(value, axis, pairs)  163 us
    all_gather x1, waiting for transfers between devices, one_gather(): lines, at, done = (lax.all_gather(flat, axis), 0, [])  66.2 us
    all_to_all x2, waiting for transfers between devices, copy_for_each(): return lax.all_to_all(copies, axis, split_axis=0, concat_axis=0, tiled=True)  59.1 us
    psum x4, blocking collectives, over_axes(): array = lax.psum(array, axis)  46.2 us
    all_to_all x7, starting transfers between devices, gather_by_exchange(): lax.all_to_all(jnp.tile(array, repeats), axis, split_axis=dim, concat_axi...  34.1 us
  transfers between devices with their start and end apart: 33, of which 26 were waited for; matrix products, arithmetic and copies ran while one was open for 8% of the time, Pallas kernels for 0%

profile of v1, /device:TPU:32, one launch (start us, length us, event | category | flops | bytes accessed | tf_op | source)
XLA Modules:
  0.0 1453.9 jit_solution(8622917416079958111)
XLA Ops:
  16.4 66.2 %all-gather.3.cloned.1.call-done = bf16[7340032]{0:T(1024)(128)(2,1)} async-done(((bf16[229376]{0:T(1024)(128)(2,1)}), bf16[7340032]{0:T(1024)(128)(2,1)}) %all-gather.3.cloned.1.call-update) | async-done | bytes 14680080 | tf_op jit(solution)/shard_map/all_gather | solution.py:47
  82.6 13.3 reshape.1416
  141.0 27.3 %all-to-all-done = bf16[4,512,1024]{2,1,0:T(8,128)(2,1)} async-done(((bf16[4,512,1024]{2,1,0:T(8,128)(2,1)}), bf16[4,512,1024]{2,1,0:T(8,128)(2,1)}, u32[]{:S(2)}, u32[]{:S(2)}) %all-to-all-start) | async-done | bytes 4194336 | tf_op jit(solution)/shard_map/all_to_all | solution.py:31
  205.8 31.9 %all-to-all-done.1 = bf16[4,512,1024]{2,1,0:T(8,128)(2,1)} async-done(((bf16[4,512,1024]{2,1,0:T(8,128)(2,1)}), bf16[4,512,1024]{2,1,0:T(8,128)(2,1)}, u32[]{:S(2)}, u32[]{:S(2)}) %all-to-all-start.1) | async-done | bytes 4194336 | tf_op jit(solution)/shard_map/all_to_all | solution.py:31
  267.1 11.7 all-to-all-done.3
  294.0 38.6 %all-to-all-done.4 = bf16[4,128,4096]{2,1,0:T(8,128)(2,1)} async-done(((bf16[4,128,4096]{2,1,0:T(8,128)(2,1)}), bf16[4,128,4096]{2,1,0:T(8,128)(2,1)}, u32[]{:S(2)}, u32[]{:S(2)}) %all-to-all-start.4) | async-done | bytes 4194336 | tf_op jit(solution)/shard_map/all_to_all | solution.py:24
  337.2 72.5 %reduce-scatter.8.cloned.1.call-done = bf16[128,4096]{1,0:T(8,128)(2,1)} async-done(((bf16[512,4096]{1,0:T(8,128)(2,1)}), bf16[128,4096]{1,0:T(8,128)(2,1)}) %reduce-scatter.8.cloned.1.call-update) | async-done | bytes 1048592 | tf_op jit(solution)/shard_map/reduce_scatter | solution.py:212
  413.7 23.3 %collective-permute-done = bf16[128,4096]{1,0:T(8,128)(2,1)S(1)} collective-permute-done((bf16[128,4096]{1,0:T(8,128)(2,1)S(1)}, bf16[128,4096]{1,0:T(8,128)(2,1)S(1)}, u32[]{:S(2)}, u32[]{:S(2)}) %collective-permute-start) | collective-permute-done | bytes 1048608 | tf_op jit(solution)/shard_map/ppermute | solution.py:58
  446.6 46.5 %all-to-all-done.5 = bf16[4,128,4096]{2,1,0:T(8,128)(2,1)} async-done(((bf16[4,128,4096]{2,1,0:T(8,128)(2,1)}), bf16[4,128,4096]{2,1,0:T(8,128)(2,1)}, u32[]{:S(2)}, u32[]{:S(2)}) %all-to-all-start.5) | async-done | bytes 4194336 | tf_op jit(solution)/shard_map/all_to_all | solution.py:24
  493.2 14.4 conditional.24
  525.3 45.0 %reduce-scatter.10.cloned.1.call-done = bf16[128,4096]{1,0:T(8,128)(2,1)} async-done(((bf16[512,4096]{1,0:T(8,128)(2,1)}), bf16[128,4096]{1,0:T(8,128)(2,1)}) %reduce-scatter.10.cloned.1.call-update) | async-done | bytes 1048592 | tf_op jit(solution)/shard_map/reduce_scatter | solution.py:212
  573.5 23.3 %collective-permute-done.2 = bf16[128,4096]{1,0:T(8,128)(2,1)S(1)} collective-permute-done((bf16[128,4096]{1,0:T(8,128)(2,1)S(1)}, bf16[128,4096]{1,0:T(8,128)(2,1)S(1)}, u32[]{:S(2)}, u32[]{:S(2)}) %collective-permute-start.2) | collective-permute-done | bytes 1048608 | tf_op jit(solution)/shard_map/ppermute | solution.py:58
  606.5 46.5 %all-to-all-done.6 = bf16[4,128,4096]{2,1,0:T(8,128)(2,1)} async-done(((bf16[4,128,4096]{2,1,0:T(8,128)(2,1)}), bf16[4,128,4096]{2,1,0:T(8,128)(2,1)}, u32[]{:S(2)}, u32[]{:S(2)}) %all-to-all-start.6) | async-done | bytes 4194336 | tf_op jit(solution)/shard_map/all_to_all | solution.py:24
  653.0 14.4 conditional.27
  667.4 10.7 conditional.28
  684.9 46.4 %reduce-scatter.12.cloned.1.call-done = bf16[128,4096]{1,0:T(8,128)(2,1)} async-done(((bf16[512,4096]{1,0:T(8,128)(2,1)}), bf16[128,4096]{1,0:T(8,128)(2,1)}) %reduce-scatter.12.cloned.1.call-update) | async-done | bytes 1048592 | tf_op jit(solution)/shard_map/reduce_scatter | solution.py:212
  734.5 23.3 %collective-permute-done.4 = bf16[128,4096]{1,0:T(8,128)(2,1)S(1)} collective-permute-done((bf16[128,4096]{1,0:T(8,128)(2,1)S(1)}, bf16[128,4096]{1,0:T(8,128)(2,1)S(1)}, u32[]{:S(2)}, u32[]{:S(2)}) %collective-permute-start.4) | collective-permute-done | bytes 1048608 | tf_op jit(solution)/shard_map/ppermute | solution.py:58
  767.5 46.5 %all-to-all-done.7 = bf16[4,128,4096]{2,1,0:T(8,128)(2,1)} async-done(((bf16[4,128,4096]{2,1,0:T(8,128)(2,1)}), bf16[4,128,4096]{2,1,0:T(8,128)(2,1)}, u32[]{:S(2)}, u32[]{:S(2)}) %all-to-all-start.7) | async-done | bytes 4194336 | tf_op jit(solution)/shard_map/all_to_all | solution.py:24
  814.0 14.6 %conditional.30 = (bf16[512,768]{0,1:T(8,128)(2,1)}) conditional(s32[]{:T(128)} %convert_element_type.543, () %tuple.154, (bf16[4,128,4096]{2,1,0:T(8,128)(2,1)}, bf16[4096,512]{0,1:T(8,128)(2,1)}, bf16[2,4096,128]{2,1,0:T(8,128)(2,1)S(1)}) %tuple.346), branch_computations={%region_44.45_spmd, %region_45.46_spmd} | conditional | flops 3226337792 | bytes 42474276 | solution.py:174
  845.9 46.4 %reduce-scatter.14.cloned.1.call-done = bf16[128,4096]{1,0:T(8,128)(2,1)} async-done(((bf16[512,4096]{1,0:T(8,128)(2,1)}), bf16[128,4096]{1,0:T(8,128)(2,1)}) %reduce-scatter.14.cloned.1.call-update) | async-done | bytes 1048592 | tf_op jit(solution)/shard_map/reduce_scatter | solution.py:212
  895.9 23.3 %collective-permute-done.6 = bf16[128,4096]{1,0:T(8,128)(2,1)S(1)} collective-permute-done((bf16[128,4096]{1,0:T(8,128)(2,1)S(1)}, bf16[128,4096]{1,0:T(8,128)(2,1)S(1)}, u32[]{:S(2)}, u32[]{:S(2)}) %collective-permute-start.6) | collective-permute-done | bytes 1048608 | tf_op jit(solution)/shard_map/ppermute | solution.py:58
  928.9 46.5 %all-to-all-done.8 = bf16[4,128,4096]{2,1,0:T(8,128)(2,1)} async-done(((bf16[4,128,4096]{2,1,0:T(8,128)(2,1)}), bf16[4,128,4096]{2,1,0:T(8,128)(2,1)}, u32[]{:S(2)}, u32[]{:S(2)}) %all-to-all-start.8) | async-done | bytes 4194336 | tf_op jit(solution)/shard_map/all_to_all | solution.py:24
  975.4 14.4 conditional.33
  1007.3 46.5 %reduce-scatter.16.cloned.1.call-done = bf16[128,4096]{1,0:T(8,128)(2,1)} async-done(((bf16[512,4096]{1,0:T(8,128)(2,1)}), bf16[128,4096]{1,0:T(8,128)(2,1)}) %reduce-scatter.16.cloned.1.call-update) | async-done | bytes 1048592 | tf_op jit(solution)/shard_map/reduce_scatter | solution.py:212
  1056.9 23.3 %collective-permute-done.8 = bf16[128,4096]{1,0:T(8,128)(2,1)S(1)} collective-permute-done((bf16[128,4096]{1,0:T(8,128)(2,1)S(1)}, bf16[128,4096]{1,0:T(8,128)(2,1)S(1)}, u32[]{:S(2)}, u32[]{:S(2)}) %collective-permute-start.8) | collective-permute-done | bytes 1048608 | tf_op jit(solution)/shard_map/ppermute | solution.py:58
  1089.9 46.5 %all-to-all-done.9 = bf16[4,128,4096]{2,1,0:T(8,128)(2,1)} async-done(((bf16[4,128,4096]{2,1,0:T(8,128)(2,1)}), bf16[4,128,4096]{2,1,0:T(8,128)(2,1)}, u32[]{:S(2)}, u32[]{:S(2)}) %all-to-all-start.9) | async-done | bytes 4194336 | tf_op jit(solution)/shard_map/all_to_all | solution.py:24
  1141.0 73.8 %reduce-scatter.18.cloned.1.call-done = bf16[128,4096]{1,0:T(8,128)(2,1)} async-done(((bf16[512,4096]{1,0:T(8,128)(2,1)}), bf16[128,4096]{1,0:T(8,128)(2,1)}) %reduce-scatter.18.cloned.1.call-update) | async-done | bytes 1048592 | tf_op jit(solution)/shard_map/reduce_scatter | solution.py:212
  1217.9 23.3 %collective-permute-done.10 = bf16[128,4096]{1,0:T(8,128)(2,1)S(1)} collective-permute-done((bf16[128,4096]{1,0:T(8,128)(2,1)S(1)}, bf16[128,4096]{1,0:T(8,128)(2,1)S(1)}, u32[]{:S(2)}, u32[]{:S(2)}) %collective-permute-start.10) | collective-permute-done | bytes 1048608 | tf_op jit(solution)/shard_map/ppermute | solution.py:58
  1250.9 46.5 %all-to-all-done.10 = bf16[4,128,4096]{2,1,0:T(8,128)(2,1)} async-done(((bf16[4,128,4096]{2,1,0:T(8,128)(2,1)}), bf16[4,128,4096]{2,1,0:T(8,128)(2,1)}, u32[]{:S(2)}, u32[]{:S(2)}) %all-to-all-start.10) | async-done | bytes 4194336 | tf_op jit(solution)/shard_map/all_to_all | solution.py:24
  1300.3 69.3 %reduce-scatter.20.cloned.1.call-done = bf16[128,4096]{1,0:T(8,128)(2,1)} async-done(((bf16[512,4096]{1,0:T(8,128)(2,1)}), bf16[128,4096]{1,0:T(8,128)(2,1)}) %reduce-scatter.20.cloned.1.call-update) | async-done | bytes 1048592 | tf_op jit(solution)/shard_map/reduce_scatter | solution.py:212
  1372.8 23.3 %collective-permute-done.12 = bf16[128,4096]{1,0:T(8,128)(2,1)S(1)} collective-permute-done((bf16[128,4096]{1,0:T(8,128)(2,1)S(1)}, bf16[128,4096]{1,0:T(8,128)(2,1)S(1)}, u32[]{:S(2)}, u32[]{:S(2)}) %collective-permute-start.12) | collective-permute-done | bytes 1048608 | tf_op jit(solution)/shard_map/ppermute | solution.py:58
  1398.3 26.3 %psum.28 = s32[]{:T(128)} all-reduce(s32[]{:T(128)} %reduce_sum.242), channel_id=1, replica_groups=mesh['section'=4,'dp_0'=4,'dp_1'=2,'mp'=4] {'section'}, use_global_device_ids=true, to_apply=%region_84.85 | all-reduce | flops 1 | bytes 8 | tf_op jit(solution)/shard_map/psum | solution.py:63
  (303 shorter events, 449.8 us)
Async XLA Ops:
  7.2 75.4 %all-gather.3.cloned.1.call-start = ((), (), s32[]{:S(2)}) async-start(), calls=%async_computation.25 | async-start | bytes 15138816 | tf_op jit(solution)/shard_map/all_gather | solution.py:47
  113.7 54.6 %all-to-all-start = ((bf16[4,512,1024]{2,1,0:T(8,128)(2,1)}), bf16[4,512,1024]{2,1,0:T(8,128)(2,1)}, u32[]{:S(2)}, u32[]{:S(2)}) async-start(bf16[4,512,1024]{2,1,0:T(8,128)(2,1)} %broadcast_in_dim.76), calls=%async_computation | async-start | bytes 8388608 | tf_op jit(solution)/shard_map/all_to_all | solution.py:31
  183.6 54.1 %all-to-all-start.1 = ((bf16[4,512,1024]{2,1,0:T(8,128)(2,1)}), bf16[4,512,1024]{2,1,0:T(8,128)(2,1)}, u32[]{:S(2)}, u32[]{:S(2)}) async-start(bf16[4,512,1024]{2,1,0:T(8,128)(2,1)} %broadcast_in_dim.85), calls=%async_computation.1 | async-start | bytes 8388608 | tf_op jit(solution)/shard_map/all_to_all | solution.py:31
  262.5 16.3 %all-to-all-start.3 = ((bf16[4,128,1024]{2,1,0:T(8,128)(2,1)}), bf16[4,128,1024]{2,1,0:T(8,128)(2,1)S(1)}, u32[]{:S(2)}, u32[]{:S(2)}) async-start(bf16[4,128,1024]{2,1,0:T(8,128)(2,1)} %bitcast.156), calls=%async_computation.3 | async-start | bytes 2097152 | tf_op jit(solution)/shard_map/all_to_all | solution.py:297
  282.5 50.1 %all-to-all-start.4 = ((bf16[4,128,4096]{2,1,0:T(8,128)(2,1)}), bf16[4,128,4096]{2,1,0:T(8,128)(2,1)}, u32[]{:S(2)}, u32[]{:S(2)}) async-start(bf16[4,128,4096]{2,1,0:T(8,128)(2,1)} %tile.14), calls=%async_computation.4 | async-start | bytes 8388608 | tf_op jit(solution)/shard_map/all_to_all | solution.py:24
  287.4 122.3 %reduce-scatter.8.cloned.1.call-start = ((), (), s32[]{:S(2)}) async-start(), calls=%async_computation.18 | async-start | bytes 5242880 | tf_op jit(solution)/shard_map/reduce_scatter | solution.py:212
  411.8 25.1 %collective-permute-start = (bf16[128,4096]{1,0:T(8,128)(2,1)S(1)}, bf16[128,4096]{1,0:T(8,128)(2,1)S(1)}, u32[]{:S(2)}, u32[]{:S(2)}) collective-permute-start(bf16[128,4096]{1,0:T(8,128)(2,1)S(1)} %fusion.241), channel_id=1, source_target_pairs={{0,32},{32,64},{64,96},{96,0},{1,33},{33,65},{65,97},{97,1},{2,34}... | collective-permute-start | bytes 3145736 | tf_op jit(solution)/shard_map/ppermute | solution.py:58
  440.1 53.1 %all-to-all-start.5 = ((bf16[4,128,4096]{2,1,0:T(8,128)(2,1)}), bf16[4,128,4096]{2,1,0:T(8,128)(2,1)}, u32[]{:S(2)}, u32[]{:S(2)}) async-start(bf16[4,128,4096]{2,1,0:T(8,128)(2,1)} %tile.15), calls=%async_computation.6 | async-start | bytes 8388608 | tf_op jit(solution)/shard_map/all_to_all | solution.py:24
  445.0 125.4 %reduce-scatter.10.cloned.1.call-start = ((), (), s32[]{:S(2)}) async-start(), calls=%async_computation.19 | async-start | bytes 5242880 | tf_op jit(solution)/shard_map/reduce_scatter | solution.py:212
  445.0 62.6 %collective-permute-start.1 = (s32[512]{0:T(512)S(1)}, s32[512]{0:T(512)S(1)}, u32[]{:S(2)}, u32[]{:S(2)}) collective-permute-start(s32[512]{0:T(512)S(1)} %bitcast.579), channel_id=1, source_target_pairs={{0,32},{32,64},{64,96},{96,0},{1,33},{33,65},{65,97},{97,1},{2,34}... | collective-permute-start | bytes 6152 | tf_op jit(solution)/shard_map/ppermute | solution.py:58
  571.9 24.9 %collective-permute-start.2 = (bf16[128,4096]{1,0:T(8,128)(2,1)S(1)}, bf16[128,4096]{1,0:T(8,128)(2,1)S(1)}, u32[]{:S(2)}, u32[]{:S(2)}) collective-permute-start(bf16[128,4096]{1,0:T(8,128)(2,1)S(1)} %fusion.240), channel_id=1, source_target_pairs={{0,32},{32,64},{64,96},{96,0},{1,33},{33,65},{65,97},{97,1},{2,34}... | collective-permute-start | bytes 3145736 | tf_op jit(solution)/shard_map/ppermute | solution.py:58
  599.9 53.1 %all-to-all-start.6 = ((bf16[4,128,4096]{2,1,0:T(8,128)(2,1)}), bf16[4,128,4096]{2,1,0:T(8,128)(2,1)}, u32[]{:S(2)}, u32[]{:S(2)}) async-start(bf16[4,128,4096]{2,1,0:T(8,128)(2,1)} %tile.16), calls=%async_computation.8 | async-start | bytes 8388608 | tf_op jit(solution)/shard_map/all_to_all | solution.py:24
  604.8 126.5 %reduce-scatter.12.cloned.1.call-start = ((), (), s32[]{:S(2)}) async-start(), calls=%async_computation.20 | async-start | bytes 5242880 | tf_op jit(solution)/shard_map/reduce_scatter | solution.py:212
  604.8 62.6 %collective-permute-start.3 = (s32[512]{0:T(512)S(1)}, s32[512]{0:T(512)S(1)}, u32[]{:S(2)}, u32[]{:S(2)}) collective-permute-start(s32[512]{0:T(512)S(1)} %collective-permute-done.1), channel_id=1, source_target_pairs={{0,32},{32,64},{64,96},{96,0},{1,33},{33,65},{65,97},{97,1},{2,34}... | collective-permute-start | bytes 6152 | tf_op jit(solution)/shard_map/ppermute | solution.py:58
  732.8 24.9 %collective-permute-start.4 = (bf16[128,4096]{1,0:T(8,128)(2,1)S(1)}, bf16[128,4096]{1,0:T(8,128)(2,1)S(1)}, u32[]{:S(2)}, u32[]{:S(2)}) collective-permute-start(bf16[128,4096]{1,0:T(8,128)(2,1)S(1)} %fusion.239), channel_id=1, source_target_pairs={{0,32},{32,64},{64,96},{96,0},{1,33},{33,65},{65,97},{97,1},{2,34}... | collective-permute-start | bytes 3145736 | tf_op jit(solution)/shard_map/ppermute | solution.py:58
  760.9 53.1 %all-to-all-start.7 = ((bf16[4,128,4096]{2,1,0:T(8,128)(2,1)}), bf16[4,128,4096]{2,1,0:T(8,128)(2,1)}, u32[]{:S(2)}, u32[]{:S(2)}) async-start(bf16[4,128,4096]{2,1,0:T(8,128)(2,1)} %tile.17), calls=%async_computation.10 | async-start | bytes 8388608 | tf_op jit(solution)/shard_map/all_to_all | solution.py:24
  765.8 126.6 %reduce-scatter.14.cloned.1.call-start = ((), (), s32[]{:S(2)}) async-start(), calls=%async_computation.21 | async-start | bytes 5242880 | tf_op jit(solution)/shard_map/reduce_scatter | solution.py:212
  765.8 62.8 %collective-permute-start.5 = (s32[512]{0:T(512)S(1)}, s32[512]{0:T(512)S(1)}, u32[]{:S(2)}, u32[]{:S(2)}) collective-permute-start(s32[512]{0:T(512)S(1)} %collective-permute-done.3), channel_id=1, source_target_pairs={{0,32},{32,64},{64,96},{96,0},{1,33},{33,65},{65,97},{97,1},{2,34}... | collective-permute-start | bytes 6152 | tf_op jit(solution)/shard_map/ppermute | solution.py:58
  893.9 25.3 %collective-permute-start.6 = (bf16[128,4096]{1,0:T(8,128)(2,1)S(1)}, bf16[128,4096]{1,0:T(8,128)(2,1)S(1)}, u32[]{:S(2)}, u32[]{:S(2)}) collective-permute-start(bf16[128,4096]{1,0:T(8,128)(2,1)S(1)} %fusion.238), channel_id=1, source_target_pairs={{0,32},{32,64},{64,96},{96,0},{1,33},{33,65},{65,97},{97,1},{2,34}... | collective-permute-start | bytes 3145736 | tf_op jit(solution)/shard_map/ppermute | solution.py:58
  922.3 53.1 %all-to-all-start.8 = ((bf16[4,128,4096]{2,1,0:T(8,128)(2,1)}), bf16[4,128,4096]{2,1,0:T(8,128)(2,1)}, u32[]{:S(2)}, u32[]{:S(2)}) async-start(bf16[4,128,4096]{2,1,0:T(8,128)(2,1)} %tile.18), calls=%async_computation.12 | async-start | bytes 8388608 | tf_op jit(solution)/shard_map/all_to_all | solution.py:24
  927.2 126.6 %reduce-scatter.16.cloned.1.call-start = ((), (), s32[]{:S(2)}) async-start(), calls=%async_computation.22 | async-start | bytes 5242880 | tf_op jit(solution)/shard_map/reduce_scatter | solution.py:212
  927.3 62.6 %collective-permute-start.7 = (s32[512]{0:T(512)S(1)}, s32[512]{0:T(512)S(1)}, u32[]{:S(2)}, u32[]{:S(2)}) collective-permute-start(s32[512]{0:T(512)S(1)} %collective-permute-done.5), channel_id=1, source_target_pairs={{0,32},{32,64},{64,96},{96,0},{1,33},{33,65},{65,97},{97,1},{2,34}... | collective-permute-start | bytes 6152 | tf_op jit(solution)/shard_map/ppermute | solution.py:58
  1055.3 24.9 %collective-permute-start.8 = (bf16[128,4096]{1,0:T(8,128)(2,1)S(1)}, bf16[128,4096]{1,0:T(8,128)(2,1)S(1)}, u32[]{:S(2)}, u32[]{:S(2)}) collective-permute-start(bf16[128,4096]{1,0:T(8,128)(2,1)S(1)} %fusion.237), channel_id=1, source_target_pairs={{0,32},{32,64},{64,96},{96,0},{1,33},{33,65},{65,97},{97,1},{2,34}... | collective-permute-start | bytes 3145736 | tf_op jit(solution)/shard_map/ppermute | solution.py:58
  1083.3 53.1 %all-to-all-start.9 = ((bf16[4,128,4096]{2,1,0:T(8,128)(2,1)}), bf16[4,128,4096]{2,1,0:T(8,128)(2,1)}, u32[]{:S(2)}, u32[]{:S(2)}) async-start(bf16[4,128,4096]{2,1,0:T(8,128)(2,1)} %tile.19), calls=%async_computation.14 | async-start | bytes 8388608 | tf_op jit(solution)/shard_map/all_to_all | solution.py:24
  1088.2 126.6 %reduce-scatter.18.cloned.1.call-start = ((), (), s32[]{:S(2)}) async-start(), calls=%async_computation.23 | async-start | bytes 5242880 | tf_op jit(solution)/shard_map/reduce_scatter | solution.py:212
  1088.3 49.1 %collective-permute-start.9 = (s32[512]{0:T(512)S(1)}, s32[512]{0:T(512)S(1)}, u32[]{:S(2)}, u32[]{:S(2)}) collective-permute-start(s32[512]{0:T(512)S(1)} %collective-permute-done.7), channel_id=1, source_target_pairs={{0,32},{32,64},{64,96},{96,0},{1,33},{33,65},{65,97},{97,1},{2,34}... | collective-permute-start | bytes 6152 | tf_op jit(solution)/shard_map/ppermute | solution.py:58
  1216.3 24.9 %collective-permute-start.10 = (bf16[128,4096]{1,0:T(8,128)(2,1)S(1)}, bf16[128,4096]{1,0:T(8,128)(2,1)S(1)}, u32[]{:S(2)}, u32[]{:S(2)}) collective-permute-start(bf16[128,4096]{1,0:T(8,128)(2,1)S(1)} %fusion.236), channel_id=1, source_target_pairs={{0,32},{32,64},{64,96},{96,0},{1,33},{33,65},{65,97},{97,1},{2,34}... | collective-permute-start | bytes 3145736 | tf_op jit(solution)/shard_map/ppermute | solution.py:58
  1244.4 53.1 %all-to-all-start.10 = ((bf16[4,128,4096]{2,1,0:T(8,128)(2,1)}), bf16[4,128,4096]{2,1,0:T(8,128)(2,1)}, u32[]{:S(2)}, u32[]{:S(2)}) async-start(bf16[4,128,4096]{2,1,0:T(8,128)(2,1)} %tile.20), calls=%async_computation.16 | async-start | bytes 8388608 | tf_op jit(solution)/shard_map/all_to_all | solution.py:24
  1249.2 120.4 %reduce-scatter.20.cloned.1.call-start = ((), (), s32[]{:S(2)}) async-start(), calls=%async_computation.24 | async-start | bytes 5242880 | tf_op jit(solution)/shard_map/reduce_scatter | solution.py:212
  1249.3 48.5 %collective-permute-start.11 = (s32[512]{0:T(512)S(1)}, s32[512]{0:T(512)S(1)}, u32[]{:S(2)}, u32[]{:S(2)}) collective-permute-start(s32[512]{0:T(512)S(1)} %collective-permute-done.9), channel_id=1, source_target_pairs={{0,32},{32,64},{64,96},{96,0},{1,33},{33,65},{65,97},{97,1},{2,34}... | collective-permute-start | bytes 6152 | tf_op jit(solution)/shard_map/ppermute | solution.py:58
  1371.2 24.9 %collective-permute-start.12 = (bf16[128,4096]{1,0:T(8,128)(2,1)S(1)}, bf16[128,4096]{1,0:T(8,128)(2,1)S(1)}, u32[]{:S(2)}, u32[]{:S(2)}) collective-permute-start(bf16[128,4096]{1,0:T(8,128)(2,1)S(1)} %fusion.235), channel_id=1, source_target_pairs={{0,32},{32,64},{64,96},{96,0},{1,33},{33,65},{65,97},{97,1},{2,34}... | collective-permute-start | bytes 3145736 | tf_op jit(solution)/shard_map/ppermute | solution.py:58
  1396.1 49.6 %collective-permute-start.13 = (bf16[128,4096]{1,0:T(8,128)(2,1)S(1)}, bf16[128,4096]{1,0:T(8,128)(2,1)S(1)}, u32[]{:S(2)}, u32[]{:S(2)}) collective-permute-start(bf16[128,4096]{1,0:T(8,128)(2,1)S(1)} %collective-permute-done.12), channel_id=1, source_target_pairs={{0,32},{32,64},{64,96},{96,0},{1,33},{33,65},{65,97},{97,1},{2,34}... | collective-permute-start | bytes 3145736 | tf_op jit(solution)/shard_map/ppermute | solution.py:58
  (22 other events, 266.2 us)
Sparse Core Ops, SparseCore 0:
  13.2 69.3 all-gather.2
  337.3 72.3 reduce-scatter.7
  525.4 44.8 reduce-scatter.9
  685.0 46.2 reduce-scatter.11
  846.0 46.2 reduce-scatter.13
  1007.4 46.2 reduce-scatter.15
  1141.1 73.6 reduce-scatter.17
  1300.4 69.1 reduce-scatter.19
